TPU v7x, 1024 devices: a whole 4x8x16 slice. The times are simulated.
1024 devices in a mesh: dp: 64 (over x, z), tensor: 8 (over y), pipe: 2 (over core).
Axes of the slice: x: 4, y: 8, z: 16, core: 2. Of those that a mesh axis runs over, the one named last changes fastest.
Arguments:
- patches: bfloat16 [1280, 49152], P('tensor', ('dp', 'pipe')), may hold values from -6 to 6
- lengths: int32 [6144], P(('dp', 'pipe')), may hold values from 1 to 8
- slot_plan: int32 [6144], P(('dp', 'pipe')), may hold values from 0 to 63, as said below
- starts: int32 [8192], P(('dp', 'pipe')), may hold values from 0 to 756, as said below
- text_rows: bfloat16 [1280, 98304], P('tensor', ('dp', 'pipe')), may hold values from -6 to 6
- cotangent: bfloat16 [1280, 98304], P('tensor', ('dp', 'pipe')), may hold values from -24 to 24
- ln_gain: float32 [1280], replicated, may hold values from 0.25 to 1.75
- ln_bias: float32 [1280], replicated, may hold values from -3 to 3
- w_qkv: bfloat16 [3, 1280, 1280], P(None, 'tensor'), may hold values from -0.15625 to 0.15625
- w_out: bfloat16 [1280, 1280], P('tensor'), may hold values from -0.15625 to 0.15625
Outputs:
- features: bfloat16 [1280, 98304], P('tensor', ('dp', 'pipe'))
- weight_grad: float32 [1280, 1280], P('tensor', ('dp', 'pipe'))
Inputs may be any that keep to these rules, and one draw needn't show every extreme that they name: `slot_plan`: the 48 images of one data group have distinct slots. `starts`: within each data group the 64 places' blocks of 8 positions rise and are disjoint, separated by 0 to 4 positions, and lie inside the group's 768 positions.
All inputs are finite; a program needn't handle non-finite values.
Results may differ from a plain program's by a relative error of at most 0.0073.
Values may be sent and summed in bfloat16 or wider, within the bound.
A program may use at most 32 MiB of HBM per device.

v0:
```python
import math

import jax
import jax.numpy as jnp
from jax import lax
from jax.sharding import Mesh
from jax.sharding import PartitionSpec as P

HEAD_DIM = 80
DP = ("dp_0", "dp_1")
DP_PIPE = ("dp_0", "dp_1", "pipe")


epsilon = 1e-06


def side_by_side(arrays, axis, split_dim, concat_dim, along):
    ends, at = ([], 0)
    for a in arrays[:-1]:
        at += a.shape[along]
        ends.append(at)
    both = jnp.concatenate(arrays, axis=along)
    return tuple(
        jnp.split(
            lax.all_to_all(both, axis, split_axis=split_dim, concat_axis=concat_dim, tiled=True),
            ends,
            axis=along,
        )
    )


def in_one_piece(arrays, axis, dim, along):
    both = jnp.concatenate(arrays, axis=along)
    out, at, gathered = (lax.all_gather(both, axis, axis=dim, tiled=True), 0, [])
    for a in arrays:
        gathered.append(lax.slice_in_dim(out, at, at + a.shape[along], axis=along))
        at += a.shape[along]
    return tuple(gathered)


def cut_along(shard, dim, peers):
    lengths = shard.shape
    pieces = shard.reshape(*lengths[:dim], peers, lengths[dim] // peers, *lengths[dim + 1 :])
    return jnp.moveaxis(pieces, dim, 0)


def summed_on_arrival(shard, axis, dim):
    peers = lax.axis_size(axis)
    pieces = lax.all_to_all(cut_along(shard, dim, peers), axis, 0, 0, tiled=True)
    return jnp.sum(pieces.astype(jnp.float32), axis=0)


def sum_in_order(pieces, axes, order):
    inside = pieces.shape[1:]
    pieces = pieces.reshape(*(lax.axis_size(a) for a in axes), *inside)
    pieces = jnp.moveaxis(pieces, order, range(len(axes))).reshape(-1, *inside)
    for k in order:
        pieces = lax.psum_scatter(pieces, axes[k], scatter_dimension=0, tiled=True)
    return pieces[0]


def scatter_axes(shard, axes, order, dim):
    peers = lax.axis_size(axes)
    return sum_in_order(cut_along(shard, dim, peers), axes, order)


def shards(
    patches, lengths, slot_plan, starts, text_rows, cotangent, ln_gain, ln_bias, w_qkv, w_out
):
    cols_here, flat_count = patches.shape
    image_count = lengths.shape[0]
    length = flat_count // image_count
    groups = lax.axis_size(DP)
    capacity = (image_count + groups - 1) // groups
    slot_total = groups * capacity
    heads_here = w_qkv.shape[1] // HEAD_DIM
    seq_rows = text_rows.shape[1]
    slot_ids = jnp.arange(slot_total, dtype=jnp.int32)
    picker = (slot_ids[:, None] == slot_plan[None, :]).astype(jnp.bfloat16)
    stacked = patches.reshape(cols_here, image_count, length)
    outgoing = jnp.einsum("si,cil->scl", picker, stacked, preferred_element_type=jnp.float32)
    outgoing = outgoing.astype(jnp.bfloat16).reshape(groups, capacity * cols_here * length)
    sizes_out = jnp.dot(
        picker, lengths.astype(jnp.bfloat16)[:, None], preferred_element_type=jnp.float32
    )
    sizes_out = sizes_out.astype(jnp.bfloat16)
    arrived, sizes_in = side_by_side((outgoing, sizes_out), DP, 0, 0, 1)
    live_len = sizes_in.reshape(slot_total).astype(jnp.int32)
    own_rows = (
        arrived.reshape(slot_total, cols_here, length)
        .transpose(1, 0, 2)
        .reshape(cols_here, slot_total * length)
    )
    offsets = jnp.arange(length, dtype=jnp.int32)
    patch_pos = jnp.minimum(starts[:, None] + offsets[None, :], seq_rows - 1).reshape(-1)
    own_cot = cotangent[:, patch_pos]
    full_rows, cot_patch = in_one_piece((own_rows, own_cot), "tensor", 0, 1)
    inputs_f = full_rows.astype(jnp.float32)
    average = jnp.mean(inputs_f, axis=0, keepdims=True)
    centred = inputs_f - average
    variance = jnp.mean(centred * centred, axis=0, keepdims=True)
    normed = (centred * lax.rsqrt(variance + epsilon) * ln_gain[:, None] + ln_bias[:, None]).astype(
        jnp.bfloat16
    )
    shape_heads = (heads_here, HEAD_DIM, slot_total, length)
    queries = (
        jnp.dot(w_qkv[0], normed, preferred_element_type=jnp.float32)
        .astype(jnp.bfloat16)
        .reshape(shape_heads)
    )
    key_rows = (
        jnp.dot(w_qkv[1], normed, preferred_element_type=jnp.float32)
        .astype(jnp.bfloat16)
        .reshape(shape_heads)
    )
    value_rows = (
        jnp.dot(w_qkv[2], normed, preferred_element_type=jnp.float32)
        .astype(jnp.bfloat16)
        .reshape(shape_heads)
    )
    scores = jnp.einsum("hesq,hesk->hsqk", queries, key_rows, preferred_element_type=jnp.float32)
    scores = scores * (1.0 / math.sqrt(HEAD_DIM))
    key_live = offsets[None, :] < jnp.maximum(live_len, 1)[:, None]
    scores = jnp.where(key_live[None, :, None, :], scores, -1e30)
    top = jnp.max(scores, axis=-1, keepdims=True)
    raised = jnp.exp(scores - top)
    weights = (raised / jnp.sum(raised, axis=-1, keepdims=True)).astype(jnp.bfloat16)
    context = jnp.einsum(
        "hsqk,hesk->hesq", weights, value_rows, preferred_element_type=jnp.float32
    ).astype(jnp.bfloat16)
    query_live = offsets[None, :] < live_len[:, None]
    context = jnp.where(query_live[None, None, :, :], context, jnp.zeros_like(context))
    context = context.reshape(heads_here * HEAD_DIM, slot_total * length)
    head_terms = lax.dot_general(
        w_out, context, (((0,), (0,)), ((), ())), preferred_element_type=jnp.float32
    )
    attended = summed_on_arrival(head_terms.astype(jnp.bfloat16), "tensor", 0).astype(jnp.bfloat16)
    merged = (own_rows.astype(jnp.float32) + attended.astype(jnp.float32)).astype(jnp.bfloat16)
    positions = jnp.arange(seq_rows, dtype=jnp.int32)[:, None]
    covered = (positions >= starts[None, :]) & (positions < starts[None, :] + live_len[None, :])
    source = jnp.sum(
        jnp.where(covered, slot_ids[None, :] * length + positions - starts[None, :], 0), axis=1
    )
    placed = merged[:, source]
    features = jnp.where(jnp.any(covered, axis=1)[None, :], placed, text_rows)
    grad_terms = lax.dot_general(
        context, cot_patch, (((1,), (1,)), ((), ())), preferred_element_type=jnp.float32
    )
    weight_grad = scatter_axes(grad_terms, DP_PIPE, (2, 1, 0), 1)
    return (features, weight_grad)


def solution(mesh):
    torus = Mesh(
        mesh.devices.reshape(4, 16, mesh.shape["tensor"], mesh.shape["pipe"]),
        ("dp_0", "dp_1", "tensor", "pipe"),
    )
    in_specs = (
        P("tensor", DP_PIPE),
        P(DP_PIPE),
        P(DP_PIPE),
        P(DP_PIPE),
        P("tensor", DP_PIPE),
        P("tensor", DP_PIPE),
        P(),
        P(),
        P(None, "tensor", None),
        P("tensor", None),
    )
    out_specs = (P("tensor", DP_PIPE), P("tensor", DP_PIPE))
    return jax.shard_map(
        shards, mesh=torus, in_specs=in_specs, out_specs=out_specs, check_vma=False
    )
```

profile of v0, /device:TPU:68, one launch (start us, length us, event | category | flops | bytes accessed | tf_op | source)
XLA Modules:
  0.0 327.2 jit_solution(8196337857853692592)
XLA Ops:
  7.2 1.1 copy.134
  8.3 1.0 convolution_convert_fusion.2
  9.3 0.2 copy.136
  9.5 0.2 fusion.21
  9.8 1.3 copy.137
  11.1 21.5 %all-to-all-start = ((bf16[64,1,1281]{2,1,0:T(2,128)(2,1)}), bf16[64,1,1281]{2,1,0:T(2,128)(2,1)S(1)}, u32[]{:S(2)}, u32[]{:S(2)}) async-start(bf16[64,1,1281]{2,1,0:T(2,128)(2,1)} %copy.137), calls=%async_computation | async-start | bytes 720896 | tf_op jit(solution)/shard_map/all_to_all | solution.py:25
  32.7 0.2 copy.140
  33.0 2.0 gather_fusion
  35.0 21.9 %all-to-all-done = bf16[64,1,1281]{2,1,0:T(2,128)(2,1)S(1)} async-done(((bf16[64,1,1281]{2,1,0:T(2,128)(2,1)}), bf16[64,1,1281]{2,1,0:T(2,128)(2,1)S(1)}, u32[]{:S(2)}, u32[]{:S(2)}) %all-to-all-start) | async-done | bytes 164000 | tf_op jit(solution)/shard_map/all_to_all | solution.py:25
  57.0 0.2 copy.138
  57.2 0.3 copy.139
  57.6 0.9 copy.141
  58.6 0.2 reduce-scatter.4.cloned.1.call-start
  58.8 0.1 convert_reduce_fusion.1
  58.9 0.6 iota_compare_fusion.5
  59.5 0.7 iota_compare_fusion.2
  60.2 41.2 %all-gather.2.cloned.1.call-done = bf16[1280,1024]{1,0:T(8,128)(2,1)} async-done(((bf16[160,1024]{1,0:T(8,128)(2,1)}), bf16[1280,1024]{1,0:T(8,128)(2,1)}) %all-gather.2.cloned.1.call-update) | async-done | bytes 2621456 | tf_op jit(solution)/shard_map/all_gather | solution.py:34
  101.4 1.7 convert_reduce_fusion
  103.1 1.7 fusion.4
  104.9 0.5 fusion.7
  105.4 0.8 copy-done.5
  106.2 1.0 fusion.16
  107.2 0.4 fusion.17
  107.6 1.1 fusion.15
  108.6 1.0 copy.143
  109.7 0.9 reshape.167
  110.6 0.1 copy.144
  110.7 0.9 reshape.168
  111.6 1.3 fusion.30
  112.9 0.8 copy.147
  113.7 0.9 fusion.48
  114.7 0.2 copy.149
  114.9 1.0 copy.142
  115.9 0.9 reshape.166
  116.8 1.2 fusion.14
  118.0 0.3 copy.150
  118.3 0.9 reshape.169
  119.2 1.2 slice.25
  120.4 2.4 dot_general.37
  122.7 2.6 fusion.10
  125.4 0.4 copy.156
  125.8 0.8 reshape.171
  126.6 0.9 copy.157
  127.4 1.5 reshape.172
  129.0 0.9 copy-done.2
  129.9 0.5 fusion.3
  130.4 1.5 copy.151
  131.9 4.3 %all-to-all-start.1 = ((bf16[8,160,512]{2,1,0:T(8,128)(2,1)}), bf16[8,160,512]{2,1,0:T(8,128)(2,1)S(1)}, u32[]{:S(2)}, u32[]{:S(2)}) async-start(bf16[8,160,512]{2,1,0:T(8,128)(2,1)} %bitcast.20), calls=%async_computation.1 | async-start | bytes 2621440 | tf_op jit(solution)/shard_map/all_to_all | solution.py:49
  136.3 1.3 dynamic-slice
  137.6 1.3 dynamic-slice.2
  138.9 0.2 copy.153
  139.7 10.6 %reduce-scatter.4.cloned.1.call-done = f32[64,160,10]{1,0,2:T(8,128)} async-done(((f32[128,160,10]{1,0,2:T(8,128)}), f32[64,160,10]{1,0,2:T(8,128)}) %reduce-scatter.4.cloned.1.call-update) | async-done | bytes 409616 | tf_op jit(solution)/shard_map/reduce_scatter | solution.py:58
  150.4 0.1 select_reduce_fusion
  150.5 0.1 fusion.35
  150.7 148.0 %all-reduce.4.cloned.1.call-done = f32[64,160,10]{1,0,2:T(8,128)} async-done(((f32[64,160,10]{1,0,2:T(8,128)}), f32[64,160,10]{1,0,2:T(8,128)}) %all-reduce.4.cloned.1.call-update) | async-done | bytes 409616
  298.7 0.9 constant_dynamic-slice_fusion.1
  299.6 15.7 %all-reduce.1 = f32[4,160,10]{1,0,2:T(4,128)S(1)} all-reduce(f32[4,160,10]{1,0,2:T(4,128)S(1)} %constant_dynamic-slice_fusion.1), channel_id=4, replica_groups=mesh['dp_0'=4,'dp_1'=16,'tensor'=8,'pipe'=2] {'dp_0'}, use_global_device_ids=true, to_apply=%region_9.10.clone | all-reduce | flops 6400 | bytes 51200
  315.3 0.7 constant_dynamic-slice_fusion
  315.9 0.6 copy.182
  316.6 0.2 reduce_sum.53
  316.8 0.1 copy.152
  317.0 2.7 gather_fusion.1
  319.6 0.2 bitcast_select_fusion
  319.8 0.8 copy.158
  (52 shorter events, 0.7 us)
Async XLA Ops:
  7.2 121.8 %copy-start = (bf16[160,1280]{1,0:T(8,128)(2,1)S(1)}, bf16[160,1280]{1,0:T(8,128)(2,1)}, u32[]{:S(2)}) copy-start(bf16[160,1280]{1,0:T(8,128)(2,1)} %param.19) | copy-start | bytes 1228804
  7.2 2.3 copy-start.14
  7.2 2.3 copy-start.15
  9.3 23.4 %copy-start.6 = (bf16[160,768]{1,0:T(8,128)(2,1)S(1)}, bf16[160,768]{1,0:T(8,128)(2,1)}, u32[]{:S(2)}) copy-start(bf16[160,768]{1,0:T(8,128)(2,1)} %param.15) | copy-start | bytes 737284
  9.7 23.1 %copy-start.10 = (s32[64]{0:T(128)S(1)}, s32[64]{0:T(128)}, u32[]{:S(2)}) copy-start(s32[64]{0:T(128)} %param.13) | copy-start | bytes 772
  11.1 45.8 %all-to-all-start = ((bf16[64,1,1281]{2,1,0:T(2,128)(2,1)}), bf16[64,1,1281]{2,1,0:T(2,128)(2,1)S(1)}, u32[]{:S(2)}, u32[]{:S(2)}) async-start(bf16[64,1,1281]{2,1,0:T(2,128)(2,1)} %copy.137), calls=%async_computation | async-start | bytes 720896 | tf_op jit(solution)/shard_map/all_to_all | solution.py:25
  32.6 68.8 %all-gather.2.cloned.1.call-start = ((), (), s32[]{:S(2)}) async-start(), calls=%async_computation.3 | async-start | bytes 2949120 | tf_op jit(solution)/shard_map/all_gather | solution.py:34
  57.5 2.7 copy-start.3
  58.6 91.7 %reduce-scatter.4.cloned.1.call-start = ((), (), s32[]{:S(2)}) async-start(), calls=%async_computation.4 | async-start | bytes 1966080 | tf_op jit(solution)/shard_map/reduce_scatter | solution.py:58
  58.9 1.3 copy-start.12
  59.5 45.3 %copy-start.9 = (f32[1280]{0:T(1024)S(1)}, f32[1280]{0:T(1024)}, u32[]{:S(2)}) copy-start(f32[1280]{0:T(1024)} %param.16) | copy-start | bytes 15364
  60.2 44.6 %copy-start.8 = (f32[1280]{0:T(1024)S(1)}, f32[1280]{0:T(1024)}, u32[]{:S(2)}) copy-start(f32[1280]{0:T(1024)} %param.17) | copy-start | bytes 15364
  101.4 3.5 %copy-start.1 = (bf16[1280,1024]{1,0:T(8,128)(2,1)S(1)}, bf16[1280,1024]{1,0:T(8,128)(2,1)}, u32[]{:S(2)}) copy-start(bf16[1280,1024]{1,0:T(8,128)(2,1)} %all-gather.2.cloned.1.call-done) | copy-start | bytes 7864324
  104.9 1.3 copy-start.5
  129.0 0.9 copy-start.2
  131.9 7.0 %copy-start.7 = (bf16[160,768]{1,0:T(8,128)(2,1)S(1)}, bf16[160,768]{1,0:T(8,128)(2,1)}, u32[]{:S(2)}) copy-start(bf16[160,768]{1,0:T(8,128)(2,1)} %param.14) | copy-start | bytes 737284
  131.9 184.7 %all-to-all-start.1 = ((bf16[8,160,512]{2,1,0:T(8,128)(2,1)}), bf16[8,160,512]{2,1,0:T(8,128)(2,1)S(1)}, u32[]{:S(2)}, u32[]{:S(2)}) async-start(bf16[8,160,512]{2,1,0:T(8,128)(2,1)} %bitcast.20), calls=%async_computation.1 | async-start | bytes 2621440 | tf_op jit(solution)/shard_map/all_to_all | solution.py:49
  136.2 14.1 %copy-start.11 = (s32[64]{0:T(128)S(1)}, s32[64]{0:T(128)}, u32[]{:S(2)}) copy-start(s32[64]{0:T(128)} %param.13) | copy-start | bytes 772
  136.3 14.1 %copy-start.13 = (s32[64]{0:T(128)S(1)}, s32[64]{0:T(128)}, u32[]{:S(2)}) copy-start(s32[64]{0:T(128)} %copy-done.12) | copy-start | bytes 772
  136.3 162.4 %all-reduce.4.cloned.1.call-start = ((), (), s32[]{:S(2)}) async-start(), calls=%async_computation.5 | async-start | bytes 1310720
  150.3 166.6 %copy-start.4 = (bf16[160,64,8]{0,2,1:T(8,128)(2,1)S(1)}, bf16[160,64,8]{0,2,1:T(8,128)(2,1)}, u32[]{:S(2)}) copy-start(bf16[160,64,8]{0,2,1:T(8,128)(2,1)} %copy-done.3) | copy-start | bytes 491524
Sparse Core Ops, SparseCore 0:
  58.7 42.6 all-gather.1
  129.1 21.1 reduce-scatter.3
  152.6 145.9 all-reduce.3
where the time goes:
time: 331 us; the launch traced here: 327 us
  waiting for transfers between devices  222 us (67%)
  local copies, waits for them, and re-layouts  32.3 us (10%)
  starting transfers between devices  26.1 us (8%)
  blocking collectives  15.7 us (5%)
  between operations  14.9 us (5%)
  matrix products  9.31 us (3%)
  other arithmetic  7.18 us (2%)
    unnamed x4, waiting for transfers between devices  148 us
    all_gather x1, waiting for transfers between devices, in_one_piece(): lax.all_gather(both, axis, axis=dim, tiled=True)  41.2 us
    all_to_all x1, waiting for transfers between devices, side_by_side(): lax.all_to_all(both, axis, split_axis=split_dim, concat_axis=concat_dim,...  21.9 us
    all_to_all x1, starting transfers between devices, side_by_side(): lax.all_to_all(both, axis, split_axis=split_dim, concat_axis=concat_dim,...  21.5 us
    unnamed x1, blocking collectives  15.7 us
    reduce_scatter x1, waiting for transfers between devices, sum_in_order(): pieces = lax.psum_scatter(pieces, axes[k], scatter_dimension=0, tiled=True)  10.6 us
    unnamed x42, local copies, waits for them, and re-layouts  8.75 us
  transfers between devices with their start and end apart: 5, of which 4 were waited for; matrix products, arithmetic and copies ran while one was open for 3% of the time, Pallas kernels for 0%

commit v1 on v0

v1 whole, which is shorter than its diff:
```python
import functools
import math

import jax
import jax.numpy as jnp
from jax import lax
from jax.experimental import pallas as pl
from jax.experimental.pallas import tpu as pltpu
from jax.sharding import PartitionSpec as P

HEAD_DIM = 80
LANES = 128
EPSILON = 1e-06
F32 = jnp.float32
BF16 = jnp.bfloat16
MESH = pl.DeviceIdType.MESH


def dot(a, b, ca=1, cb=0):
    return lax.dot_general(a, b, (((ca,), (cb,)), ((), ())), preferred_element_type=F32)


def iota(shape, dim):
    return lax.broadcasted_iota(jnp.int32, shape, dim)


def kernel(
    g,
    patches_hbm,
    text_hbm,
    cot_hbm,
    wqkv_hbm,
    wout_hbm,
    lengths_ref,
    slots_ref,
    starts_ref,
    gain_ref,
    bias_ref,
    features_ref,
    grad_ref,
    patches,
    text,
    cot,
    wqkv,
    wout,
    xfull,
    cfull,
    w_split,
    w_full,
    onehot,
    pick,
    gainb,
    biasb,
    cot_out,
    cot_in,
    cot_sel,
    merged_out,
    merged_in,
    grad_own,
    pair_out,
    pair_in,
    row_out,
    row_in,
    col_out,
    col_in,
    load_sem,
    xs_sem,
    xr_sem,
    cs_sem,
    cr_sem,
    a2a_send,
    a2a_recv,
    w_send,
    w_recv,
    pair_send,
    pair_recv,
    row_send,
    row_recv,
    col_send,
    col_recv,
):
    nx, nz, ny = g.nx, g.nz, g.ny
    ndp = nx * nz
    rows, width, chunks = g.rows, g.width, g.chunks
    cols = width * chunks
    length = g.length
    slots = ndp * length
    dp, y, c = lax.axis_index("dp"), lax.axis_index("tensor"), lax.axis_index("pipe")
    x, z = dp // nz, lax.rem(dp, nz)
    other = 1 - c

    loads = [
        pltpu.make_async_copy(a, b, load_sem.at[k])
        for k, (a, b) in enumerate(
            (
                (patches_hbm, patches),
                (cot_hbm, cot),
                (wout_hbm, wout),
                (wqkv_hbm, wqkv),
                (text_hbm, text),
            )
        )
    ]
    for load in loads:
        load.start()

    def plane_peer(k):
        return (
            lax.rem(x + k // nz, nx) * nz + lax.rem(z + lax.rem(k + nz // 2, nz), nz),
            y,
            c,
        )

    barrier = pltpu.get_barrier_semaphore()

    def greet(device):
        pl.semaphore_signal(barrier, inc=1, device_id=device, device_id_type=MESH)

    for k in range(1, ny):
        greet((dp, lax.rem(y + k, ny), c))
    greet((dp, y, other))

    def greet_plane(k, carry):
        greet(plane_peer(k))
        return carry

    lax.fori_loop(0, nz // 2, greet_plane, 0)
    lax.fori_loop(nz // 2 + 1, ndp, greet_plane, 0)
    per_t = ndp // ny
    per_x = ny // nx
    source_x = lax.rem(y // per_x + nx // 2, nx)
    source_y = dp // per_t

    def greet_source(k, carry):
        greet((source_x * nz + k, source_y, c))
        return carry

    lax.fori_loop(0, nz, greet_source, 0)
    pl.semaphore_wait(barrier, ny - 1 + 1 + ndp - 1 + nz)

    half = ny // 2
    limits = [(half, ny - 1 - half) if ch % 2 == 0 else (ny - 1 - half, half) for ch in range(chunks)]

    def hop(buf, ssem, rsem, way, step, ch):
        if way == 0:
            origin, peer = lax.rem(y + ny - step, ny), lax.rem(y + 1, ny)
        else:
            origin, peer = lax.rem(y + step, ny), lax.rem(y + ny - 1, ny)
        return pltpu.make_async_remote_copy(
            src_ref=buf.at[ch, origin],
            dst_ref=buf.at[ch, origin],
            send_sem=ssem.at[way, step, ch],
            recv_sem=rsem.at[way, step, ch],
            device_id=(dp, peer, c),
            device_id_type=MESH,
        )

    hop_x = functools.partial(hop, xfull, xs_sem, xr_sem)
    hop_c = functools.partial(hop, cfull, cs_sem, cr_sem)

    def open_ring(hops, ch):
        for way in range(2):
            if limits[ch][way] > 0:
                hops(way, 0, ch).start()

    def turn(hops, step, ch):
        for way in range(2):
            if step < limits[ch][way]:
                hops(way, step, ch).wait_recv()
                if step + 1 < limits[ch][way]:
                    hops(way, step + 1, ch).start()

    def close_ring(hops):
        for ch in range(chunks):
            for way in range(2):
                for step in range(limits[ch][way]):
                    hops(way, step, ch).wait_send()

    def exchange(send, recv, k):
        def start(n, carry):
            peer = plane_peer(n)
            pltpu.make_async_remote_copy(
                src_ref=send.at[peer[0]],
                dst_ref=recv.at[dp],
                send_sem=a2a_send.at[k],
                recv_sem=a2a_recv.at[k],
                device_id=peer,
                device_id_type=MESH,
            ).start()
            return carry

        lax.fori_loop(0, nz // 2, start, 0)
        lax.fori_loop(nz // 2 + 1, ndp, start, 0)
        recv[dp] = send[dp]

    def exchanged(send, recv, k):
        part = pl.ds(0, ndp - 1)
        pltpu.make_async_copy(recv.at[part], recv.at[part], a2a_recv.at[k]).wait()
        pltpu.make_async_copy(send.at[part], send.at[part], a2a_send.at[k]).wait()

    loads[0].wait()
    for ch in range(chunks):
        xfull[ch, y] = patches[:, ch * width : (ch + 1) * width]
        open_ring(hop_x, ch)

    place = iota((slots, ndp), 0) // length == iota((slots, ndp), 1)
    position = jnp.sum(
        jnp.where(place, starts_ref[...].astype(F32), 0.0), axis=1, keepdims=True
    ).astype(jnp.int32) + lax.rem(iota((slots, 1), 0), length)
    seq = g.seq
    onehot[...] = (iota((slots, seq), 1) == position).astype(F32).astype(BF16)
    loads[1].wait()
    each, room = g.each, LANES // per_t
    lined = iota((2 * LANES, rows), 0)
    rest = lax.rem(lined, LANES)
    column = (rest // room * 2 + lined // LANES) * each + lax.rem(rest, room)
    order = ((lax.rem(rest, room) < each) & (column == iota((2 * LANES, rows), 1))).astype(F32).astype(BF16)
    cot_lined = dot(order, cot[...]).astype(BF16)
    pair = [
        dot(onehot[...], cot_lined[k * LANES : (k + 1) * LANES], 1, 1).reshape(ndp, length, LANES)
        for k in range(2)
    ]
    cot_out[...] = jnp.concatenate(pair, axis=1).astype(BF16)
    exchange(cot_out, cot_in, 0)

    for ch in range(chunks):
        turn(hop_x, 0, ch)
    loads[2].wait()
    w_split[...] = wout[...].T.reshape(w_split.shape)
    for ch in range(chunks):
        turn(hop_x, 1, ch) if ny > 2 else None
    gainb[...] = jnp.broadcast_to(gain_ref[...], (width, rows * ny)).T
    biasb[...] = jnp.broadcast_to(bias_ref[...], (width, rows * ny)).T
    images = cols // length
    spread = (iota((images, cols), 1) // length == iota((images, cols), 0)).astype(F32).astype(BF16)

    def per_column(ref):
        values = jnp.broadcast_to(ref[...].astype(F32), (8, images)).astype(BF16)
        return dot(values, spread)[0:1].astype(jnp.int32)

    live_len = per_column(lengths_ref)
    within = lax.rem(iota((1, cols), 1), length)
    target = per_column(slots_ref) * length + within
    live = within < live_len
    pick[...] = (iota((slots, cols), 0) == target).astype(F32).astype(BF16)
    for step in range(2, half - 1):
        for ch in range(chunks):
            turn(hop_x, step, ch)

    def w_copy(k):
        peer = lax.rem(y + k, ny)
        return pltpu.make_async_remote_copy(
            src_ref=w_split.at[peer, c],
            dst_ref=w_full.at[c, y],
            send_sem=w_send.at[0],
            recv_sem=w_recv.at[0],
            device_id=(dp, peer, c),
            device_id_type=MESH,
        )

    for k in sorted(range(1, ny), key=lambda k: -min(k, ny - k)):
        w_copy(k).start()
    w_full[c, y] = w_split[y, c]
    w_pair = pltpu.make_async_remote_copy(
        src_ref=w_full.at[c],
        dst_ref=w_full.at[c],
        send_sem=w_send.at[1],
        recv_sem=w_recv.at[1],
        device_id=(dp, y, other),
        device_id_type=MESH,
    )

    loads[3].wait()
    key_row, query_col = iota((width, width), 0), iota((width, width), 1)
    same = key_row // length == query_col // length
    for ch in range(chunks):
        if ny > 2:
            turn(hop_x, half - 1, ch)
        here = slice(ch * width, (ch + 1) * width)
        inputs = xfull[ch].reshape(ny * rows, width).astype(F32)
        centred = inputs - jnp.mean(inputs, axis=0, keepdims=True)
        variance = jnp.mean(centred * centred, axis=0, keepdims=True)
        normed = (centred * lax.rsqrt(variance + EPSILON) * gainb[...] + biasb[...]).astype(BF16)
        queries, keys, values = (dot(wqkv[k], normed).astype(BF16) for k in range(3))
        mask = same & (lax.rem(key_row, length) < live_len[:, here])
        contexts = []
        for head in range(rows // HEAD_DIM):
            part = slice(head * HEAD_DIM, (head + 1) * HEAD_DIM)
            scores = dot(keys[part], queries[part], 0, 0) * (1.0 / math.sqrt(HEAD_DIM))
            scores = jnp.where(mask, scores, -1e30)
            raised = jnp.exp(scores - jnp.max(scores, axis=0, keepdims=True))
            weights = (raised / jnp.sum(raised, axis=0, keepdims=True)).astype(BF16)
            contexts.append(dot(values[part], weights))
        context = jnp.concatenate(contexts, axis=0)
        cfull[ch, y] = jnp.where(live[:, here], context, 0.0).astype(BF16)
        open_ring(hop_c, ch)
    close_ring(hop_x)

    exchanged(cot_out, cot_in, 0)
    arrived = cot_in[...].astype(F32)
    for k in range(2):
        block = arrived[:, k * length : (k + 1) * length].reshape(slots, LANES).astype(BF16)
        cot_sel[k] = dot(block, pick[...], 0, 0).astype(BF16)

    for ch in range(chunks):
        turn(hop_c, 0, ch)
    part = pl.ds(0, ny - 1)
    pltpu.make_async_copy(w_full.at[c, part], w_full.at[c, part], w_recv.at[0]).wait()
    pltpu.make_async_copy(w_full.at[c, part], w_full.at[c, part], w_send.at[0]).wait()
    w_pair.start()
    for step in range(1, half):
        for ch in range(chunks):
            turn(hop_c, step, ch)
    w_pair.wait()

    pieces = []
    for ch in range(chunks):
        here = slice(ch * width, (ch + 1) * width)
        attended = jnp.zeros((rows, width), F32)
        for t in range(ny):
            block = jnp.concatenate([w_full[0, t], w_full[1, t]], axis=0)
            attended += dot(block, cfull[ch, t]).astype(BF16).astype(F32)
        merged = patches[:, here].astype(F32) + attended.astype(BF16).astype(F32)
        alive = jnp.where(live[:, here] & (iota((2 * LANES - rows, width), 0) == 0), 1.0, 0.0)
        pieces.append(jnp.concatenate([merged, alive], axis=0).astype(BF16))
    merged = jnp.concatenate(pieces, axis=1)
    pair = [
        dot(pick[...], merged[k * LANES : (k + 1) * LANES], 1, 1).reshape(ndp, length, LANES)
        for k in range(2)
    ]
    merged_out[...] = jnp.concatenate(pair, axis=1).astype(BF16)
    exchange(merged_out, merged_in, 1)

    def term(k):
        total = jnp.zeros((ny * rows, LANES), F32)
        for ch in range(chunks):
            block = cot_sel[k, :, ch * width : (ch + 1) * width]
            total += dot(cfull[ch].reshape(ny * rows, width), block, 1, 1)
        return total

    pair_out[...] = term(other).astype(pair_out.dtype)
    pair_copy = pltpu.make_async_remote_copy(
        src_ref=pair_out,
        dst_ref=pair_in,
        send_sem=pair_send,
        recv_sem=pair_recv,
        device_id=(dp, y, other),
        device_id_type=MESH,
    )
    pair_copy.start()
    grad_own[...] = term(c).reshape(grad_own.shape)
    pair_copy.wait()
    grad_own[...] += pair_in[...].astype(F32).reshape(grad_own.shape)
    row_out[...] = grad_own[...].astype(BF16)
    row_copies = []
    for k in range(1, nx):
        peer = lax.rem(x + k, nx)
        row_copies.append(
            pltpu.make_async_remote_copy(
                src_ref=row_out.at[lax.rem(peer + nx // 2, nx)],
                dst_ref=row_in.at[k - 1],
                send_sem=row_send.at[k - 1],
                recv_sem=row_recv.at[k - 1],
                device_id=(peer * nz + z, y, c),
                device_id_type=MESH,
            )
        )
        row_copies[-1].start()
    share = lax.rem(x + nx // 2, nx)
    total = grad_own[share]
    for k, copy in enumerate(row_copies):
        copy.wait()
        total += row_in[k].astype(F32)
    for b in range(per_x):
        turned = total[b * rows : (b + 1) * rows].T
        col_out[b] = turned.reshape(per_t, room, rows).astype(BF16)

    def send_column(k, carry):
        b, target = k // per_t, lax.rem(k, per_t)
        pltpu.make_async_remote_copy(
            src_ref=col_out.at[b, target],
            dst_ref=col_in.at[z],
            send_sem=col_send,
            recv_sem=col_recv,
            device_id=(y * per_t + target, share * per_x + b, c),
            device_id_type=MESH,
        ).start()
        return carry

    lax.fori_loop(0, per_x * per_t, send_column, 0)
    close_ring(hop_c)

    exchanged(merged_out, merged_in, 1)
    loads[4].wait()
    arrived = merged_in[...].astype(F32)
    first = arrived[:, :length].reshape(slots, LANES).T.astype(BF16)
    second = arrived[:, length:].reshape(slots, LANES).T.astype(BF16)
    over = rows - LANES
    wide = g.seq_block
    for k in range(seq // wide):
        here = slice(k * wide, (k + 1) * wide)
        spots = onehot[:, here]
        upper, lower = dot(first, spots), dot(second, spots)
        covered = lower[over : over + 1] > 0.5
        placed = jnp.concatenate([upper, lower[:over]], axis=0).astype(BF16)
        features_ref[:, here] = jnp.where(covered, placed, text[:, here])

    pltpu.make_async_copy(col_in, col_in, col_recv).wait()
    pltpu.make_async_copy(col_out, col_out, col_send).wait()
    total = jnp.sum(col_in[...].astype(F32), axis=0)
    grad_ref[...] = total.T[:, :each]


class Geometry:
    def __init__(self, nx, nz, ny, rows, cols, images, seq):
        self.nx, self.nz, self.ny, self.rows = nx, nz, ny, rows
        self.length = cols // images
        self.chunks = 3
        self.width = cols // self.chunks
        self.seq = seq
        self.seq_block = 256 if seq % 256 == 0 else seq
        self.each = rows * ny // (nx * nz * 2)


def shards(nx, patches, lengths, slot_plan, starts, text_rows, cotangent, ln_gain, ln_bias, w_qkv, w_out):
    ndp, ny = lax.axis_size("dp"), lax.axis_size("tensor")
    rows, cols = patches.shape
    d = w_out.shape[1]
    seq = text_rows.shape[1]
    g = Geometry(nx, ndp // nx, ny, rows, cols, lengths.shape[0], seq)
    slots = ndp * g.length
    per_t, per_x, room = ndp // ny, ny // nx, LANES // (ndp // ny)
    half = max(ny // 2, 1)
    hbm, vmem = pl.BlockSpec(memory_space=pl.ANY), pl.BlockSpec(memory_space=pltpu.VMEM)
    dma = pltpu.SemaphoreType.DMA
    ring = (g.chunks, ny, rows, g.width)
    packets = (ndp, 2 * g.length, LANES)
    scratch = [
        pltpu.VMEM(patches.shape, BF16),
        pltpu.VMEM(text_rows.shape, BF16),
        pltpu.VMEM(cotangent.shape, BF16),
        pltpu.VMEM(w_qkv.shape, BF16),
        pltpu.VMEM(w_out.shape, BF16),
        pltpu.VMEM(ring, BF16),
        pltpu.VMEM(ring, BF16),
        pltpu.VMEM((ny, 2, rows // 2, rows), BF16),
        pltpu.VMEM((2, ny, rows // 2, rows), BF16),
        pltpu.VMEM((slots, seq), BF16),
        pltpu.VMEM((slots, cols), BF16),
        pltpu.VMEM((d, g.width), F32),
        pltpu.VMEM((d, g.width), F32),
        pltpu.VMEM(packets, BF16),
        pltpu.VMEM(packets, BF16),
        pltpu.VMEM((2, LANES, cols), BF16),
        pltpu.VMEM(packets, BF16),
        pltpu.VMEM(packets, BF16),
        pltpu.VMEM((nx, d // nx, LANES), F32),
        pltpu.VMEM((d, LANES), F32),
        pltpu.VMEM((d, LANES), F32),
        pltpu.VMEM((nx, d // nx, LANES), BF16),
        pltpu.VMEM((nx - 1, d // nx, LANES), BF16),
        pltpu.VMEM((per_x, per_t, room, rows), BF16),
        pltpu.VMEM((g.nz, room, rows), BF16),
        dma((5,)),
        dma((2, half, g.chunks)),
        dma((2, half, g.chunks)),
        dma((2, half, g.chunks)),
        dma((2, half, g.chunks)),
        dma((2,)),
        dma((2,)),
        dma((2,)),
        dma((2,)),
        dma,
        dma,
        dma((nx - 1,)),
        dma((nx - 1,)),
        dma,
        dma,
    ]
    return pl.pallas_call(
        functools.partial(kernel, g),
        out_shape=(
            jax.ShapeDtypeStruct(text_rows.shape, BF16),
            jax.ShapeDtypeStruct((rows, g.each), F32),
        ),
        in_specs=[hbm] * 5 + [vmem] * 5,
        out_specs=(vmem, vmem),
        scratch_shapes=scratch,
        compiler_params=pltpu.CompilerParams(collective_id=0, has_side_effects=True, vmem_limit_bytes=48 << 20),
    )(
        patches,
        text_rows,
        cotangent,
        w_qkv,
        w_out,
        lengths.reshape(1, -1),
        slot_plan.reshape(1, -1),
        starts.reshape(1, -1),
        ln_gain.reshape(1, -1),
        ln_bias.reshape(1, -1),
    )


def solution(mesh, nx=4):
    groups = ("dp", "pipe")
    in_specs = (
        P("tensor", groups),
        P(groups),
        P(groups),
        P(groups),
        P("tensor", groups),
        P("tensor", groups),
        P(),
        P(),
        P(None, "tensor", None),
        P("tensor", None),
    )
    out_specs = (P("tensor", groups), P("tensor", groups))
    return jax.shard_map(
        functools.partial(shards, nx), mesh=mesh, in_specs=in_specs, out_specs=out_specs, check_vma=False
    )
```

time: 331 us -> 102 us (0.31)
  the two profiles are of different devices: /device:TPU:68 before, /device:TPU:72 now
where the time goes in v1:
time: 102 us
  Pallas kernels  91.5 us (90%)
  local copies, waits for them, and re-layouts  9.82 us (10%)
    pallas_call x1, Pallas kernels, shards(): pl.pallas_call(functools.partial(kernel, g), out_shape=(jax.ShapeDtypeStr...  91.5 us
    unnamed x17, local copies, waits for them, and re-layouts  7.73 us

profile of v1, /device:TPU:72, one launch (start us, length us, event | category | flops | bytes accessed | tf_op | source)
XLA Modules:
  0.0 102.0 jit_solution(17285785293771650072)
XLA Ops:
  0.6 0.7 reshape.22.gain_ref
  1.3 0.7 reshape.23.bias_ref
  2.0 0.0 copy-start
  2.0 1.3 %copy-done = bf16[3,160,1280]{2,1,0:T(8,128)(2,1)S(1)} copy-done((bf16[3,160,1280]{2,1,0:T(8,128)(2,1)S(1)}, bf16[3,160,1280]{2,1,0:T(8,128)(2,1)}, u32[]{:S(2)}) %copy-start) | copy-done | bytes 1228824
  3.3 0.0 copy-start.1
  3.3 1.0 copy-done.1
  4.3 0.0 copy-start.2
  4.3 0.9 copy-done.2
  5.3 0.0 copy-start.3
  5.3 0.9 copy-done.3
  6.2 0.0 copy-start.4
  6.2 0.9 copy-done.4
  7.1 0.0 copy-start.5
  7.1 0.7 copy-done.5
  7.8 0.0 copy-start.6
  7.8 0.7 copy-done.6
  8.4 0.0 copy-start.7
  8.4 0.7 copy-done.7
  9.1 91.5 %shard_map.113 = (bf16[160,768]{1,0:T(8,128)(2,1)S(1)}, f32[160,10]{1,0:T(8,128)S(1)}) custom-call(bf16[160,384]{1,0:T(8,128)(2,1)S(1)} %copy-done.4, bf16[160,768]{1,0:T(8,128)(2,1)S(1)} %copy-done.2, bf16[160,768]{1,0:T(8,128)(2,1)S(1)} %copy-done.3, bf16[3,160,1280]{2,1,0:T(8,128)(2,1)S(1)} %copy-done, bf16[160,1280]{1,0:T(8,128)(2,1)S(1)} %copy-done.1, ...), custom_call_target="tpu_custom_call" | custom-call | tf_op jit(solution)/shard_map/pallas_call | solution.py:480
  100.6 0.7 copy.12
  101.3 0.7 copy.14
Async XLA Ops:
  2.0 1.3 %copy-start = (bf16[3,160,1280]{2,1,0:T(8,128)(2,1)S(1)}, bf16[3,160,1280]{2,1,0:T(8,128)(2,1)}, u32[]{:S(2)}) copy-start(bf16[3,160,1280]{2,1,0:T(8,128)(2,1)} %wqkv_hbm.1) | copy-start | bytes 3686404
  3.3 1.0 copy-start.1
  4.3 0.9 copy-start.2
  5.3 0.9 copy-start.3
  6.2 0.9 copy-start.4
  7.1 0.7 copy-start.5
  7.8 0.7 copy-start.6
  8.4 0.7 copy-start.7

commit v2 on v1

v2 whole, which is shorter than its diff:
```python
import functools
import math

import jax
import jax.numpy as jnp
from jax import lax
from jax.experimental import pallas as pl
from jax.experimental.pallas import tpu as pltpu
from jax.sharding import PartitionSpec as P

HEAD_DIM = 80
LANES = 128
EPSILON = 1e-06
F32 = jnp.float32
BF16 = jnp.bfloat16
MESH = pl.DeviceIdType.MESH


def dot(a, b, ca=1, cb=0):
    return lax.dot_general(a, b, (((ca,), (cb,)), ((), ())), preferred_element_type=F32)


def iota(shape, dim):
    return lax.broadcasted_iota(jnp.int32, shape, dim)


def kernel(
    g,
    patches_hbm,
    text_hbm,
    cot_hbm,
    wqkv_hbm,
    wout_hbm,
    lengths_hbm,
    slots_hbm,
    starts_hbm,
    gain_hbm,
    bias_hbm,
    features_ref,
    grad_ref,
    patches,
    text,
    cot,
    wqkv,
    wout,
    lengths_ref,
    slots_ref,
    starts_ref,
    gain_ref,
    bias_ref,
    xfull,
    cfull,
    w_split,
    w_full,
    onehot,
    pick,
    gainb,
    biasb,
    cot_out,
    cot_in,
    cot_sel,
    merged_out,
    merged_in,
    attended,
    grad_own,
    pair_out,
    pair_in,
    row_out,
    row_in,
    col_out,
    col_in,
    near_sem,
    load_sem,
    xs_sem,
    xr_sem,
    cs_sem,
    cr_sem,
    a2a_send,
    a2a_recv,
    w_send,
    w_recv,
    pair_send,
    pair_recv,
    row_send,
    row_recv,
    col_send,
    col_recv,
):
    nx, nz, ny = g.nx, g.nz, g.ny
    ndp = nx * nz
    rows, width, chunks = g.rows, g.width, g.chunks
    cols = width * chunks
    length = g.length
    slots = ndp * length
    dp, y, c = lax.axis_index("dp"), lax.axis_index("tensor"), lax.axis_index("pipe")
    x, z = dp // nz, lax.rem(dp, nz)
    other = 1 - c

    loads = [
        pltpu.make_async_copy(a, b, load_sem.at[k])
        for k, (a, b) in enumerate(
            (
                (patches_hbm, patches),
                (cot_hbm, cot),
                (wout_hbm, wout),
                (wqkv_hbm, wqkv),
                (text_hbm, text),
                (lengths_hbm, lengths_ref.at[0]),
                (slots_hbm, slots_ref.at[0]),
                (starts_hbm, starts_ref.at[0]),
                (gain_hbm, gain_ref.at[0]),
                (bias_hbm, bias_ref.at[0]),
            )
        )
    ]
    for load in loads:
        load.start()

    def plane_peer(k):
        return (
            lax.rem(x + k // nz, nx) * nz + lax.rem(z + lax.rem(k + nz // 2, nz), nz),
            y,
            c,
        )

    phase = Phase()
    phase('greet')
    barrier = pltpu.get_barrier_semaphore()

    def signal(sem, device):
        pl.semaphore_signal(sem, inc=1, device_id=device, device_id_type=MESH)

    def place_at(dx, dz):
        return (lax.rem(x + dx, nx) * nz + lax.rem(z + dz, nz), y, c)

    signal(barrier, (dp, y, other))
    for way in (1, -1):
        signal(barrier, (dp, lax.rem(y + ny + way, ny), c))
        signal(barrier, place_at(0, nz + way))
        signal(barrier, place_at(nx + way, 0))
    phase('barrier_wait')
    pl.semaphore_wait(barrier, 7)

    rounds = []
    for count, axis in ((nz, 1), (nx, 0)):
        reach = 1
        while reach < count // 2:
            step = [(count + reach), (count - reach)]
            rounds.append([(0, r) if axis else (r, 0) for r in step])
            reach *= 2
    rounds.append([(r, 0) for r in range(1, nx)])

    def knock(n):
        for dx, dz in rounds[n]:
            signal(near_sem.at[n], place_at(dx, dz))

    def hear(n):
        pl.semaphore_wait(near_sem.at[n], len(rounds[n]))

    half = ny // 2
    parts = 2
    tall = rows // parts
    units = [(ch, h) for ch in range(chunks) for h in range(parts)]
    limits = {u: (half, ny - 1 - half) if n % 2 == 0 else (ny - 1 - half, half) for n, u in enumerate(units)}

    def hop(buf, ssem, rsem, way, step, unit):
        ch, h = unit
        if way == 0:
            origin, peer = lax.rem(y + ny - step, ny), lax.rem(y + 1, ny)
        else:
            origin, peer = lax.rem(y + step, ny), lax.rem(y + ny - 1, ny)
        piece = buf.at[ch, origin, pl.ds(h * tall, tall)]
        n = ch * parts + h
        return pltpu.make_async_remote_copy(
            src_ref=piece,
            dst_ref=piece,
            send_sem=ssem.at[way, step, n],
            recv_sem=rsem.at[way, step, n],
            device_id=(dp, peer, c),
            device_id_type=MESH,
        )

    hop_x = functools.partial(hop, xfull, xs_sem, xr_sem)
    hop_c = functools.partial(hop, cfull, cs_sem, cr_sem)

    def open_ring(hops, ch):
        for h in range(parts):
            for way in range(2):
                if limits[ch, h][way] > 0:
                    hops(way, 0, (ch, h)).start()

    def turn(hops, step, ch):
        for h in range(parts):
            for way in range(2):
                if step < limits[ch, h][way]:
                    hops(way, step, (ch, h)).wait_recv()
                    if step + 1 < limits[ch, h][way]:
                        hops(way, step + 1, (ch, h)).start()

    def close_ring(hops):
        for unit in units:
            for way in range(2):
                for step in range(limits[unit][way]):
                    hops(way, step, unit).wait_send()

    def exchange(send, recv, k, low, high):
        count = high - low
        if count == 0:
            return

        def start(n, carry):
            peer = place_at(n // count, low + lax.rem(n, count))
            pltpu.make_async_remote_copy(
                src_ref=send.at[peer[0]],
                dst_ref=recv.at[dp],
                send_sem=a2a_send.at[k],
                recv_sem=a2a_recv.at[k],
                device_id=peer,
                device_id_type=MESH,
            ).start()
            return carry

        lax.fori_loop(0 if low % nz else 1, nx * count, start, 0)

    def exchanged(send, recv, k):
        part = pl.ds(0, ndp - 1)
        pltpu.make_async_copy(recv.at[part], recv.at[part], a2a_recv.at[k]).wait()
        pltpu.make_async_copy(send.at[part], send.at[part], a2a_send.at[k]).wait()

    phase('open_x')
    loads[0].wait()
    for ch in range(chunks):
        xfull[ch, y] = patches[:, ch * width : (ch + 1) * width]
        open_ring(hop_x, ch)
    z_rounds = 0
    while 2 ** (z_rounds + 1) <= nz // 2:
        z_rounds += 1
    last_round = len(rounds) - 1
    if z_rounds:
        knock(0)
    for n in range(z_rounds, last_round):
        knock(n)

    phase('cot_out')
    for load in loads[5:]:
        load.wait()
    place = iota((slots, ndp), 0) // length == iota((slots, ndp), 1)
    position = jnp.sum(
        jnp.where(place, starts_ref[...].astype(F32), 0.0), axis=1, keepdims=True
    ).astype(jnp.int32) + lax.rem(iota((slots, 1), 0), length)
    seq = g.seq
    onehot[...] = (iota((slots, seq), 1) == position).astype(F32).astype(BF16)
    loads[1].wait()
    each, room = g.each, LANES // g.per_t
    lined = iota((2 * LANES, rows), 0)
    rest = lax.rem(lined, LANES)
    column = (rest // room * 2 + lined // LANES) * each + lax.rem(rest, room)
    order = ((lax.rem(rest, room) < each) & (column == iota((2 * LANES, rows), 1))).astype(F32).astype(BF16)
    cot_lined = dot(order, cot[...]).astype(BF16)
    pair = [
        dot(onehot[...], cot_lined[k * LANES : (k + 1) * LANES], 1, 1).reshape(ndp, length, LANES)
        for k in range(2)
    ]
    cot_out[...] = jnp.concatenate(pair, axis=1).astype(BF16)
    cot_in[dp] = cot_out[dp]

    images = cols // length
    spread = (iota((images, cols), 1) // length == iota((images, cols), 0)).astype(F32).astype(BF16)

    def per_column(ref):
        values = jnp.broadcast_to(ref[...].astype(F32), (8, images)).astype(BF16)
        return dot(values, spread)[0:1].astype(jnp.int32)

    live_len = per_column(lengths_ref)
    within = lax.rem(iota((1, cols), 1), length)
    target = per_column(slots_ref) * length + within
    live = within < live_len

    def turn_weights():
        loads[2].wait()
        w_split[...] = wout[...].T.reshape(w_split.shape)
        w_full[c, y] = w_split[y, c]

    def spread_norm():
        gainb[...] = jnp.broadcast_to(gain_ref[...], (width, rows * ny)).T
        biasb[...] = jnp.broadcast_to(bias_ref[...], (width, rows * ny)).T

    def build_pick():
        pick[...] = (iota((slots, cols), 0) == target).astype(F32).astype(BF16)

    tasks = [turn_weights, spread_norm, build_pick]
    heard = 0

    def next_round():
        nonlocal heard
        if heard < z_rounds:
            hear(heard)
            heard += 1
            if heard < z_rounds:
                knock(heard)
        if heard == z_rounds:
            for n in range(z_rounds, last_round):
                hear(n)
            knock(last_round)
            heard += 1

    for step in range(half - 1):
        phase('turn_x%d' % step)
        for ch in range(chunks):
            turn(hop_x, step, ch)
        next_round()
        if tasks:
            tasks.pop(0)()
    phase('rounds')
    for task in tasks:
        task()
    while heard <= z_rounds:
        next_round()

    def w_copy(k):
        peer = lax.rem(y + k, ny)
        return pltpu.make_async_remote_copy(
            src_ref=w_split.at[peer, c],
            dst_ref=w_full.at[c, y],
            send_sem=w_send.at[0],
            recv_sem=w_recv.at[0],
            device_id=(dp, peer, c),
            device_id_type=MESH,
        )

    far_first = sorted(range(1, ny), key=lambda k: -min(k, ny - k))
    for k in far_first:
        if k != half:
            w_copy(k).start()
    w_pair = pltpu.make_async_remote_copy(
        src_ref=w_full.at[c],
        dst_ref=w_full.at[c],
        send_sem=w_send.at[1],
        recv_sem=w_recv.at[1],
        device_id=(dp, y, other),
        device_id_type=MESH,
    )
    hear(last_round)
    phase('cot_send')
    near = max(nz // 4, 1)
    exchange(cot_out, cot_in, 0, near, nz - near + 1)
    exchange(cot_out, cot_in, 0, nz - near + 1, nz)
    exchange(cot_out, cot_in, 0, 0, near)

    loads[3].wait()
    key_row, query_col = iota((width, width), 0), iota((width, width), 1)
    same = key_row // length == query_col // length
    for ch in range(chunks):
        phase('turn_x_last_%d' % ch)
        turn(hop_x, half - 1, ch)
        if ch == 0:
            w_copy(half).start()
        phase('attention_%d' % ch)
        here = slice(ch * width, (ch + 1) * width)
        inputs = xfull[ch].reshape(ny * rows, width).astype(F32)
        centred = inputs - jnp.mean(inputs, axis=0, keepdims=True)
        variance = jnp.mean(centred * centred, axis=0, keepdims=True)
        normed = (centred * lax.rsqrt(variance + EPSILON) * gainb[...] + biasb[...]).astype(BF16)
        queries, keys, values = (dot(wqkv[k], normed).astype(BF16) for k in range(3))
        mask = same & (lax.rem(key_row, length) < live_len[:, here])
        contexts = []
        for head in range(rows // HEAD_DIM):
            part = slice(head * HEAD_DIM, (head + 1) * HEAD_DIM)
            scores = dot(keys[part], queries[part], 0, 0) * (1.0 / math.sqrt(HEAD_DIM))
            scores = jnp.where(mask, scores, -1e30)
            raised = jnp.exp(scores - jnp.max(scores, axis=0, keepdims=True))
            weights = (raised / jnp.sum(raised, axis=0, keepdims=True)).astype(BF16)
            contexts.append(dot(values[part], weights))
        context = jnp.concatenate(contexts, axis=0)
        cfull[ch, y] = jnp.where(live[:, here], context, 0.0).astype(BF16)
        open_ring(hop_c, ch)
    phase('close_x')
    close_ring(hop_x)

    arrivals = [0]
    for away in range(1, half + 1):
        arrivals += [away, ny - away] if away < half else [away]
    per_x = g.per_x
    shares = [arrivals[k * per_x : (k + 1) * per_x] for k in range(nx)]
    ready = [max(max(min(a, ny - a) for a in share) - 1, 0) for share in shares]
    home_x = y * g.per_t // nz
    mine = lax.rem(x + nx - home_x + nx // 2, nx)

    def block_at(away):
        return lax.rem(y + away, ny)

    def project(away):
        at = block_at(away)
        weights = jnp.concatenate([w_full[0, at], w_full[1, at]], axis=0)
        for ch in range(chunks):
            piece = dot(weights, cfull[ch, at]).astype(BF16).astype(F32)
            attended[ch] = piece if away == 0 else attended[ch] + piece

    def pair_copy(k):
        return pltpu.make_async_remote_copy(
            src_ref=pair_out.at[k],
            dst_ref=pair_in.at[k],
            send_sem=pair_send.at[k],
            recv_sem=pair_recv.at[k],
            device_id=(dp, y, other),
            device_id_type=MESH,
        )

    def term(k, side):
        blocks = []
        for away in shares[k]:
            total = jnp.zeros((rows, LANES), F32)
            for ch in range(chunks):
                block = cot_sel[side, :, ch * width : (ch + 1) * width]
                total += dot(cfull[ch, block_at(away)], block, 1, 1)
            blocks.append(total)
        return jnp.concatenate(blocks, axis=0)

    def first_stage(k):
        pair_out[k] = term(k, other)
        pair_copy(k).start()
        grad_own[k] = term(k, c)

    def row_copy(k):
        peer = lax.rem(home_x + k + nx - nx // 2, nx)
        slot = lax.rem(peer - x + nx + nx - 1, nx)
        return pltpu.make_async_remote_copy(
            src_ref=row_out.at[k],
            dst_ref=row_in.at[slot],
            send_sem=row_send.at[k],
            recv_sem=row_recv.at[slot],
            device_id=(peer * nz + z, y, c),
            device_id_type=MESH,
        )

    def second_stage(k):
        pair_copy(k).wait()
        total = grad_own[k] + pair_in[k]
        grad_own[k] = total
        row_out[k] = total.astype(BF16)

        @pl.when(mine != k)
        def _():
            row_copy(k).start()

    def column_copy(b, target, away):
        return pltpu.make_async_remote_copy(
            src_ref=col_out.at[b, target],
            dst_ref=col_in.at[z],
            send_sem=col_send,
            recv_sem=col_recv,
            device_id=(y * g.per_t + target, block_at(away), c),
            device_id_type=MESH,
        )

    over = rows - LANES

    def third_stage(k):
        @pl.when(mine == k)
        def _():
            total = grad_own[k]
            for slot in range(nx - 1):
                arrived = pltpu.make_async_copy(row_in.at[slot], row_in.at[slot], row_recv.at[slot])
                arrived.wait()
                total += row_in[slot].astype(F32)
            for b, away in enumerate(shares[k]):
                turned = total[b * rows : (b + 1) * rows].T.reshape(g.per_t, room, rows)
                tail = turned[:, :each, LANES:]
                spare = jnp.zeros((g.per_t, each // 2, LANES - 2 * over), F32)
                tail = jnp.concatenate([tail[:, : each // 2], tail[:, each // 2 :], spare], axis=2)
                spare = jnp.zeros((g.per_t, room - each - each // 2, LANES), F32)
                packed = jnp.concatenate([turned[:, :each, :LANES], tail, spare], axis=1)
                col_out[b] = packed.astype(BF16)

                def send(target, carry, b=b, away=away):
                    column_copy(b, target, away).start()
                    return carry

                lax.fori_loop(0, g.per_t, send, 0)

    def select_cotangent():
        exchanged(cot_out, cot_in, 0)
        arrived = cot_in[...].astype(F32)
        for k in range(2):
            block = arrived[:, k * length : (k + 1) * length].reshape(slots, LANES).astype(BF16)
            cot_sel[k] = dot(block, pick[...], 0, 0).astype(BF16)

    begun, paired, ended, projected = 0, 0, 0, 0
    working = min(1, half - 1)
    for step in range(half):
        phase('turn_c%d' % step)
        for ch in range(chunks):
            turn(hop_c, step, ch)
        phase('work_c%d' % step)
        if step == 0:
            part = pl.ds(0, ny - 1)
            pltpu.make_async_copy(w_full.at[c, part], w_full.at[c, part], w_recv.at[0]).wait()
            pltpu.make_async_copy(w_full.at[c, part], w_full.at[c, part], w_send.at[0]).wait()
            w_pair.start()
        if step == working:
            phase('cot_wait')
            w_pair.wait()
            select_cotangent()
            phase('work_c%d' % step)
        if step < working:
            continue
        fresh = [k for k in range(begun, nx) if ready[k] <= step]
        for k in fresh:
            first_stage(k)
        while projected < ny and min(arrivals[projected], ny - arrivals[projected]) <= step + 1:
            project(arrivals[projected])
            projected += 1
        before = paired
        for k in range(paired, begun):
            second_stage(k)
            paired += 1
        for k in range(ended, before):
            third_stage(k)
            ended += 1
        begun += len(fresh)
        if step == half - 1:
            before = paired if paired < nx - 1 else nx - 2
            for k in range(ended, min(before, 2)):
                third_stage(k)
                ended += 1

    phase('merged_out')
    pieces = []
    for ch in range(chunks):
        here = slice(ch * width, (ch + 1) * width)
        merged = patches[:, here].astype(F32) + attended[ch].astype(BF16).astype(F32)
        alive = jnp.where(live[:, here] & (iota((2 * LANES - rows, width), 0) == 0), 1.0, 0.0)
        pieces.append(jnp.concatenate([merged, alive], axis=0).astype(BF16))
    merged = jnp.concatenate(pieces, axis=1)
    pair = [
        dot(pick[...], merged[k * LANES : (k + 1) * LANES], 1, 1).reshape(ndp, length, LANES)
        for k in range(2)
    ]
    merged_out[...] = jnp.concatenate(pair, axis=1).astype(BF16)
    merged_in[dp] = merged_out[dp]
    phase('pair_last')
    for k in range(paired, nx):
        second_stage(k)
    phase('merged_send')
    exchange(merged_out, merged_in, 1, near, nz - near + 1)
    phase('third')
    for k in range(ended, nx):
        third_stage(k)
    phase('merged_send2')
    exchange(merged_out, merged_in, 1, nz - near + 1, nz)
    exchange(merged_out, merged_in, 1, 0, near)
    close_ring(hop_c)
    for k in range(nx):
        @pl.when(mine != k)
        def _(k=k):
            row_copy(k).wait_send()

    phase('merged_wait')
    exchanged(merged_out, merged_in, 1)
    phase('place')
    loads[4].wait()
    arrived = merged_in[...].astype(F32)
    first = arrived[:, :length].reshape(slots, LANES).T.astype(BF16)
    second = arrived[:, length:].reshape(slots, LANES).T.astype(BF16)
    wide = g.seq_block
    for k in range(seq // wide):
        here = slice(k * wide, (k + 1) * wide)
        spots = onehot[:, here]
        upper, lower = dot(first, spots), dot(second, spots)
        covered = lower[over : over + 1] > 0.5
        placed = jnp.concatenate([upper, lower[:over]], axis=0).astype(BF16)
        features_ref[:, here] = jnp.where(covered, placed, text[:, here])

    phase('col_wait')
    pltpu.make_async_copy(col_in, col_in, col_recv).wait()
    pltpu.make_async_copy(col_out, col_out, col_send).wait()
    phase('finish')
    total = jnp.sum(col_in[...].astype(F32), axis=0)
    tail = total[each : each + each // 2]
    tail = jnp.concatenate([tail[:, :over], tail[:, over : 2 * over]], axis=0)
    grad_ref[...] = jnp.concatenate([total[:each], tail], axis=1)
    phase(None)


class Phase:
    scope = None

    def __call__(self, name):
        if self.scope is not None:
            self.scope.__exit__(None, None, None)
        self.scope = jax.named_scope(name) if name else None
        if name:
            self.scope.__enter__()


class Geometry:
    def __init__(self, nx, nz, ny, rows, cols, images, seq):
        self.nx, self.nz, self.ny, self.rows = nx, nz, ny, rows
        self.length = cols // images
        self.chunks = 3
        self.width = cols // self.chunks
        self.seq = seq
        self.seq_block = 256 if seq % 256 == 0 else seq
        self.per_t, self.per_x = nx * nz // ny, ny // nx
        self.each = rows * ny // (nx * nz * 2)


def shards(nx, patches, lengths, slot_plan, starts, text_rows, cotangent, ln_gain, ln_bias, w_qkv, w_out):
    ndp, ny = lax.axis_size("dp"), lax.axis_size("tensor")
    rows, cols = patches.shape
    d = w_out.shape[1]
    seq = text_rows.shape[1]
    g = Geometry(nx, ndp // nx, ny, rows, cols, lengths.shape[0], seq)
    slots = ndp * g.length
    room = LANES // g.per_t
    half = max(ny // 2, 1)
    hbm, vmem = pl.BlockSpec(memory_space=pl.ANY), pl.BlockSpec(memory_space=pltpu.VMEM)
    dma = pltpu.SemaphoreType.DMA
    ring = (g.chunks, ny, rows, g.width)
    packets = (ndp, 2 * g.length, LANES)
    scratch = [
        pltpu.VMEM(patches.shape, BF16),
        pltpu.VMEM(text_rows.shape, BF16),
        pltpu.VMEM(cotangent.shape, BF16),
        pltpu.VMEM(w_qkv.shape, BF16),
        pltpu.VMEM(w_out.shape, BF16),
        pltpu.VMEM((1,) + lengths.shape, jnp.int32),
        pltpu.VMEM((1,) + slot_plan.shape, jnp.int32),
        pltpu.VMEM((1,) + starts.shape, jnp.int32),
        pltpu.VMEM((1,) + ln_gain.shape, F32),
        pltpu.VMEM((1,) + ln_bias.shape, F32),
        pltpu.VMEM(ring, BF16),
        pltpu.VMEM(ring, BF16),
        pltpu.VMEM((ny, 2, rows // 2, rows), BF16),
        pltpu.VMEM((2, ny, rows // 2, rows), BF16),
        pltpu.VMEM((slots, seq), BF16),
        pltpu.VMEM((slots, cols), BF16),
        pltpu.VMEM((d, g.width), F32),
        pltpu.VMEM((d, g.width), F32),
        pltpu.VMEM(packets, BF16),
        pltpu.VMEM(packets, BF16),
        pltpu.VMEM((2, LANES, cols), BF16),
        pltpu.VMEM(packets, BF16),
        pltpu.VMEM(packets, BF16),
        pltpu.VMEM((g.chunks, rows, g.width), F32),
        pltpu.VMEM((nx, d // nx, LANES), F32),
        pltpu.VMEM((nx, d // nx, LANES), F32),
        pltpu.VMEM((nx, d // nx, LANES), F32),
        pltpu.VMEM((nx, d // nx, LANES), BF16),
        pltpu.VMEM((nx - 1, d // nx, LANES), BF16),
        pltpu.VMEM((g.per_x, g.per_t, room, LANES), BF16),
        pltpu.VMEM((g.nz, room, LANES), BF16),
        pltpu.SemaphoreType.REGULAR((8,)),
        dma((10,)),
        dma((2, half, 2 * g.chunks)),
        dma((2, half, 2 * g.chunks)),
        dma((2, half, 2 * g.chunks)),
        dma((2, half, 2 * g.chunks)),
        dma((2,)),
        dma((2,)),
        dma((2,)),
        dma((2,)),
        dma((nx,)),
        dma((nx,)),
        dma((nx,)),
        dma((nx - 1,)),
        dma,
        dma,
    ]
    features, grad = pl.pallas_call(
        functools.partial(kernel, g),
        out_shape=(
            jax.ShapeDtypeStruct(text_rows.shape, BF16),
            jax.ShapeDtypeStruct((g.each, rows), F32),
        ),
        in_specs=[hbm] * 10,
        out_specs=(vmem, vmem),
        scratch_shapes=scratch,
        compiler_params=pltpu.CompilerParams(collective_id=0, has_side_effects=True),
    )(
        patches,
        text_rows,
        cotangent,
        w_qkv,
        w_out,
        lengths,
        slot_plan,
        starts,
        ln_gain,
        ln_bias,
    )
    return features, grad.T


def solution(mesh, nx=4):
    groups = ("dp", "pipe")
    in_specs = (
        P("tensor", groups),
        P(groups),
        P(groups),
        P(groups),
        P("tensor", groups),
        P("tensor", groups),
        P(),
        P(),
        P(None, "tensor", None),
        P("tensor", None),
    )
    out_specs = (P("tensor", groups), P("tensor", groups))
    return jax.shard_map(
        functools.partial(shards, nx), mesh=mesh, in_specs=in_specs, out_specs=out_specs, check_vma=False
    )
```

time: 102 us -> 83 us (0.81)
  the two profiles are of different devices: /device:TPU:72 before, /device:TPU:68 now
where the time goes in v2:
time: 83 us; the launch traced here: 82.7 us
  Pallas kernels  79.1 us (95%)
  local copies, waits for them, and re-layouts  2.98 us (4%)
    pallas_call x1, Pallas kernels, shards(): pl.pallas_call(functools.partial(kernel, g), out_shape=(jax.ShapeDtypeStr...  79.1 us
    unnamed x2, local copies, waits for them, and re-layouts  2.98 us

profile of v2, /device:TPU:68, one launch (start us, length us, event | category | flops | bytes accessed | tf_op | source)
XLA Modules:
  0.0 82.7 jit_solution(6091614447379243580)
XLA Ops:
  0.6 79.1 %shard_map.113 = (bf16[160,768]{1,0:T(8,128)(2,1)}, f32[10,160]{1,0:T(8,128)}) custom-call(bf16[160,384]{1,0:T(8,128)(2,1)} %patches_hbm.1, bf16[160,768]{1,0:T(8,128)(2,1)} %text_hbm.1, bf16[160,768]{1,0:T(8,128)(2,1)} %cot_hbm.1, bf16[3,160,1280]{2,1,0:T(8,128)(2,1)} %wqkv_hbm.1, bf16[160,1280]{1,0:T(8,128)(2,1)} %wout_hbm.1, s32[48]{0:T(128)} %lengths_hbm.1, ...), custom_call_target="tpu_custom_call" | custom-call | tf_op jit(solution)/shard_map/pallas_call | solution.py:670
  79.8 1.7 %copy.14 = bf16[160,768]{1,0:T(8,128)(2,1)} copy(bf16[160,768]{1,0:T(8,128)(2,1)} %get-tuple-element.8) | data formatting | bytes 491520
  81.4 1.3 %copy.15 = f32[160,10]{0,1:T(8,128)} copy(f32[160,10]{0,1:T(8,128)} %bitcast.1) | data formatting | bytes 12800

commit v3 on v2

--- a/solution.py
+++ b/solution.py
@@ -36,8 +36,8 @@
     starts_hbm,
     gain_hbm,
     bias_hbm,
-    features_ref,
-    grad_ref,
+    features_hbm,
+    grad_hbm,
     patches,
     text,
     cot,
@@ -69,6 +69,16 @@
     row_in,
     col_out,
     col_in,
+    features,
+    grad,
+    low_out,
+    low_in,
+    onehot_low,
+    pick_low,
+    cover,
+    store_sem,
+    low_send,
+    low_recv,
     near_sem,
     load_sem,
     xs_sem,
@@ -203,29 +213,37 @@
                 for step in range(limits[unit][way]):
                     hops(way, step, unit).wait_send()
 
-    def exchange(send, recv, k, low, high):
+    def exchange(arrays, low, high):
         count = high - low
         if count == 0:
             return
 
         def start(n, carry):
             peer = place_at(n // count, low + lax.rem(n, count))
-            pltpu.make_async_remote_copy(
-                src_ref=send.at[peer[0]],
-                dst_ref=recv.at[dp],
-                send_sem=a2a_send.at[k],
-                recv_sem=a2a_recv.at[k],
-                device_id=peer,
-                device_id_type=MESH,
-            ).start()
+            for send, recv, sent, got in arrays:
+                pltpu.make_async_remote_copy(
+                    src_ref=send.at[peer[0]],
+                    dst_ref=recv.at[dp],
+                    send_sem=sent,
+                    recv_sem=got,
+                    device_id=peer,
+                    device_id_type=MESH,
+                ).start()
             return carry
 
         lax.fori_loop(0 if low % nz else 1, nx * count, start, 0)
 
-    def exchanged(send, recv, k):
+    def exchanged(arrays):
         part = pl.ds(0, ndp - 1)
-        pltpu.make_async_copy(recv.at[part], recv.at[part], a2a_recv.at[k]).wait()
-        pltpu.make_async_copy(send.at[part], send.at[part], a2a_send.at[k]).wait()
+        for send, recv, sent, got in arrays:
+            pltpu.make_async_copy(recv.at[part], recv.at[part], got).wait()
+            pltpu.make_async_copy(send.at[part], send.at[part], sent).wait()
+
+    cot_arrays = ((cot_out, cot_in, a2a_send.at[0], a2a_recv.at[0]),)
+    image_arrays = (
+        (merged_out, merged_in, a2a_send.at[1], a2a_recv.at[1]),
+        (low_out, low_in, low_send, low_recv),
+    )
 
     phase('open_x')
     loads[0].wait()
@@ -250,6 +268,25 @@
     ).astype(jnp.int32) + lax.rem(iota((slots, 1), 0), length)
     seq = g.seq
     onehot[...] = (iota((slots, seq), 1) == position).astype(F32).astype(BF16)
+    place = lax.rem(iota((slots, ndp), 0), ndp) == iota((slots, ndp), 1)
+    position = jnp.sum(
+        jnp.where(place, starts_ref[...].astype(F32), 0.0), axis=1, keepdims=True
+    ).astype(jnp.int32) + iota((slots, 1), 0) // ndp
+    onehot_low[...] = (iota((slots, seq), 1) == position).astype(F32).astype(BF16)
+
+    images = cols // length
+    spread = (iota((images, cols), 1) // length == iota((images, cols), 0)).astype(F32).astype(BF16)
+
+    def per_column(ref):
+        values = jnp.broadcast_to(ref[...].astype(F32), (8, images)).astype(BF16)
+        return dot(values, spread)[0:1].astype(jnp.int32)
+
+    live_len = per_column(lengths_ref)
+    within = lax.rem(iota((1, cols), 1), length)
+    slot_of = per_column(slots_ref)
+    live = within < live_len
+    pick[...] = (iota((slots, cols), 0) == slot_of * length + within).astype(F32).astype(BF16)
+    pick_low[...] = (iota((ndp, cols), 0) == slot_of).astype(F32).astype(BF16)
     loads[1].wait()
     each, room = g.each, LANES // g.per_t
     lined = iota((2 * LANES, rows), 0)
@@ -261,67 +298,74 @@
         dot(onehot[...], cot_lined[k * LANES : (k + 1) * LANES], 1, 1).reshape(ndp, length, LANES)
         for k in range(2)
     ]
+    flags = jnp.broadcast_to(jnp.where(live, 1.0, 0.0), (LANES, cols)).astype(BF16)
+    flags = dot(pick[...], flags, 1, 1).reshape(ndp, length, LANES)
+    pair[0] = jnp.where(iota((ndp, length, LANES), 2) == room - 1, flags, pair[0])
     cot_out[...] = jnp.concatenate(pair, axis=1).astype(BF16)
     cot_in[dp] = cot_out[dp]
 
-    images = cols // length
-    spread = (iota((images, cols), 1) // length == iota((images, cols), 0)).astype(F32).astype(BF16)
-
-    def per_column(ref):
-        values = jnp.broadcast_to(ref[...].astype(F32), (8, images)).astype(BF16)
-        return dot(values, spread)[0:1].astype(jnp.int32)
-
-    live_len = per_column(lengths_ref)
-    within = lax.rem(iota((1, cols), 1), length)
-    target = per_column(slots_ref) * length + within
-    live = within < live_len
+    side = lax.rem(z, 2)
 
     def turn_weights():
         loads[2].wait()
         w_split[...] = wout[...].T.reshape(w_split.shape)
-        w_full[c, y] = w_split[y, c]
+        w_full[c, side, y] = w_split[y, c, side]
 
     def spread_norm():
         gainb[...] = jnp.broadcast_to(gain_ref[...], (width, rows * ny)).T
         biasb[...] = jnp.broadcast_to(bias_ref[...], (width, rows * ny)).T
 
-    def build_pick():
-        pick[...] = (iota((slots, cols), 0) == target).astype(F32).astype(BF16)
-
-    tasks = [turn_weights, spread_norm, build_pick]
-    heard = 0
-
-    def next_round():
-        nonlocal heard
-        if heard < z_rounds:
-            hear(heard)
-            heard += 1
-            if heard < z_rounds:
-                knock(heard)
-        if heard == z_rounds:
-            for n in range(z_rounds, last_round):
-                hear(n)
+    def hear_axes():
+        for n in range(z_rounds, last_round):
+            hear(n)
+
+    def next_round(n):
+        hear(n)
+        if n + 1 < z_rounds:
+            knock(n + 1)
+        else:
+            hear_axes()
             knock(last_round)
-            heard += 1
+
+    near = max(nz // 4, 1)
+
+    def send_cotangent():
+        hear(last_round)
+        exchange(cot_arrays, near, nz - near + 1)
+
+    def send_cotangent_rest():
+        exchange(cot_arrays, nz - near + 1, nz)
+        exchange(cot_arrays, 0, near)
+
+    if z_rounds:
+        next_round(0)
+    else:
+        hear_axes()
+        knock(last_round)
+    tasks = [turn_weights, None, spread_norm, None]
+    for n in range(1, z_rounds):
+        tasks[2 * n - 1] = functools.partial(next_round, n)
+    tasks += [send_cotangent, send_cotangent_rest]
 
     for step in range(half - 1):
-        phase('turn_x%d' % step)
         for ch in range(chunks):
+            phase('turn_x%d' % step)
             turn(hop_x, step, ch)
-        next_round()
-        if tasks:
-            tasks.pop(0)()
-    phase('rounds')
+            if tasks:
+                task = tasks.pop(0)
+                phase('task_x%d_%d' % (step, ch))
+                if task:
+                    task()
+    phase('rest_x')
     for task in tasks:
-        task()
-    while heard <= z_rounds:
-        next_round()
+        if task:
+            task()
 
     def w_copy(k):
         peer = lax.rem(y + k, ny)
         return pltpu.make_async_remote_copy(
-            src_ref=w_split.at[peer, c],
-            dst_ref=w_full.at[c, y],
+            src_ref=w_split.at[peer, c, side],
+            dst_ref=w_full.at[c, side, y],
             send_sem=w_send.at[0],
             recv_sem=w_recv.at[0],
             device_id=(dp, peer, c),
@@ -332,6 +376,14 @@
     for k in far_first:
         if k != half:
             w_copy(k).start()
+    w_beside = pltpu.make_async_remote_copy(
+        src_ref=w_full.at[c, side],
+        dst_ref=w_full.at[c, side],
+        send_sem=w_send.at[2],
+        recv_sem=w_recv.at[2],
+        device_id=(dp + 1 - 2 * side, y, c),
+        device_id_type=MESH,
+    )
     w_pair = pltpu.make_async_remote_copy(
         src_ref=w_full.at[c],
         dst_ref=w_full.at[c],
@@ -340,13 +392,6 @@
         device_id=(dp, y, other),
         device_id_type=MESH,
     )
-    hear(last_round)
-    phase('cot_send')
-    near = max(nz // 4, 1)
-    exchange(cot_out, cot_in, 0, near, nz - near + 1)
-    exchange(cot_out, cot_in, 0, nz - near + 1, nz)
-    exchange(cot_out, cot_in, 0, 0, near)
-
     loads[3].wait()
     key_row, query_col = iota((width, width), 0), iota((width, width), 1)
     same = key_row // length == query_col // length
@@ -391,7 +436,7 @@
 
     def project(away):
         at = block_at(away)
-        weights = jnp.concatenate([w_full[0, at], w_full[1, at]], axis=0)
+        weights = jnp.concatenate([w_full[k // 2, k % 2, at] for k in range(4)], axis=0)
         for ch in range(chunks):
             piece = dot(weights, cfull[ch, at]).astype(BF16).astype(F32)
             attended[ch] = piece if away == 0 else attended[ch] + piece
@@ -479,76 +524,91 @@
                 lax.fori_loop(0, g.per_t, send, 0)
 
     def select_cotangent():
-        exchanged(cot_out, cot_in, 0)
+        exchanged(cot_arrays)
         arrived = cot_in[...].astype(F32)
         for k in range(2):
             block = arrived[:, k * length : (k + 1) * length].reshape(slots, LANES).astype(BF16)
             cot_sel[k] = dot(block, pick[...], 0, 0).astype(BF16)
 
-    begun, paired, ended, projected = 0, 0, 0, 0
-    working = min(1, half - 1)
+    def find_cover():
+        block = cot_in[...].astype(F32)[:, :length].reshape(slots, LANES).T
+        cover[...] = dot(block[room - 8 : room].astype(BF16), onehot[...])
+
+    def take_weights():
+        mine_only = w_full.at[c, side, pl.ds(0, ny - 1)]
+        pltpu.make_async_copy(mine_only, mine_only, w_recv.at[0]).wait()
+        pltpu.make_async_copy(mine_only, mine_only, w_send.at[0]).wait()
+        w_beside.start()
+
+    def pair_weights():
+        w_beside.wait()
+        w_pair.start()
+
+    def between(k):
+        def run():
+            second_stage(k - 1)
+            if k == 1:
+                w_pair.wait()
+            for away in shares[k - 1]:
+                project(away)
+
+        return run
+
+    tasks = [(-1, take_weights), (0, None), (0, select_cotangent), (ready[0], functools.partial(first_stage, 0))]
+    tasks.append((0, pair_weights))
+    for k in range(1, nx):
+        tasks += [(ready[k], functools.partial(first_stage, k)), (ready[k], between(k))]
     for step in range(half):
-        phase('turn_c%d' % step)
         for ch in range(chunks):
+            phase('turn_c%d' % step)
             turn(hop_c, step, ch)
-        phase('work_c%d' % step)
-        if step == 0:
-            part = pl.ds(0, ny - 1)
-            pltpu.make_async_copy(w_full.at[c, part], w_full.at[c, part], w_recv.at[0]).wait()
-            pltpu.make_async_copy(w_full.at[c, part], w_full.at[c, part], w_send.at[0]).wait()
-            w_pair.start()
-        if step == working:
-            phase('cot_wait')
-            w_pair.wait()
-            select_cotangent()
-            phase('work_c%d' % step)
-        if step < working:
-            continue
-        fresh = [k for k in range(begun, nx) if ready[k] <= step]
-        for k in fresh:
-            first_stage(k)
-        while projected < ny and min(arrivals[projected], ny - arrivals[projected]) <= step + 1:
-            project(arrivals[projected])
-            projected += 1
-        before = paired
-        for k in range(paired, begun):
-            second_stage(k)
-            paired += 1
-        for k in range(ended, before):
-            third_stage(k)
-            ended += 1
-        begun += len(fresh)
-        if step == half - 1:
-            before = paired if paired < nx - 1 else nx - 2
-            for k in range(ended, min(before, 2)):
-                third_stage(k)
-                ended += 1
+            done = step if ch == chunks - 1 else step - 1
+            if tasks and tasks[0][0] <= done and (step < half - 1 or ch < chunks - 1):
+                phase('task_c%d_%d' % (step, ch))
+                task = tasks.pop(0)[1]
+                if task:
+                    task()
+    phase('rest_c')
+    for _, task in tasks:
+        if task:
+            task()
+    for away in shares[-1]:
+        project(away)
+    for k in range(nx - 2):
+        phase('third_%d' % k)
+        third_stage(k)
 
     phase('merged_out')
     pieces = []
     for ch in range(chunks):
         here = slice(ch * width, (ch + 1) * width)
         merged = patches[:, here].astype(F32) + attended[ch].astype(BF16).astype(F32)
-        alive = jnp.where(live[:, here] & (iota((2 * LANES - rows, width), 0) == 0), 1.0, 0.0)
-        pieces.append(jnp.concatenate([merged, alive], axis=0).astype(BF16))
+        pieces.append(merged.astype(BF16))
     merged = jnp.concatenate(pieces, axis=1)
-    pair = [
-        dot(pick[...], merged[k * LANES : (k + 1) * LANES], 1, 1).reshape(ndp, length, LANES)
-        for k in range(2)
-    ]
-    merged_out[...] = jnp.concatenate(pair, axis=1).astype(BF16)
+    upper = dot(pick[...], merged[:LANES], 1, 1).reshape(ndp, length, LANES)
+    merged_out[...] = upper.astype(BF16)
+    group = LANES // over
+    for r in range(2):
+        spots = [
+            jnp.where(within == r * group + q, merged[LANES:].astype(F32), 0.0).astype(BF16)
+            for q in range(group)
+        ]
+        low_out[:, r, :] = dot(pick_low[...], jnp.concatenate(spots, axis=0), 1, 1)
     merged_in[dp] = merged_out[dp]
+    low_in[dp] = low_out[dp]
     phase('pair_last')
-    for k in range(paired, nx):
-        second_stage(k)
+    second_stage(nx - 1)
     phase('merged_send')
-    exchange(merged_out, merged_in, 1, near, nz - near + 1)
-    phase('third')
-    for k in range(ended, nx):
-        third_stage(k)
+    exchange(image_arrays, near, nz - near + 1)
+    phase('third_last')
+    third_stage(nx - 2)
+    third_stage(nx - 1)
     phase('merged_send2')
-    exchange(merged_out, merged_in, 1, nz - near + 1, nz)
-    exchange(merged_out, merged_in, 1, 0, near)
+    exchange(image_arrays, nz - near + 1, nz)
+    exchange(image_arrays, 0, near)
+    phase('cover')
+    find_cover()
+    loads[4].wait()
     close_ring(hop_c)
     for k in range(nx):
         @pl.when(mine != k)
@@ -556,20 +616,25 @@
             row_copy(k).wait_send()
 
     phase('merged_wait')
-    exchanged(merged_out, merged_in, 1)
+    exchanged(image_arrays)
     phase('place')
-    loads[4].wait()
-    arrived = merged_in[...].astype(F32)
-    first = arrived[:, :length].reshape(slots, LANES).T.astype(BF16)
-    second = arrived[:, length:].reshape(slots, LANES).T.astype(BF16)
+    first = merged_in[...].astype(F32).reshape(slots, LANES).T.astype(BF16)
+    second = [
+        low_in[:, j // group, :][:, j % group * over : (j % group + 1) * over] for j in range(length)
+    ]
+    second = jnp.concatenate(second, axis=0).T.astype(BF16)
     wide = g.seq_block
+    stores = []
     for k in range(seq // wide):
         here = slice(k * wide, (k + 1) * wide)
-        spots = onehot[:, here]
-        upper, lower = dot(first, spots), dot(second, spots)
-        covered = lower[over : over + 1] > 0.5
-        placed = jnp.concatenate([upper, lower[:over]], axis=0).astype(BF16)
-        features_ref[:, here] = jnp.where(covered, placed, text[:, here])
+        upper, lower = dot(first, onehot[:, here]), dot(second, onehot_low[:, here])
+        placed = jnp.concatenate([upper, lower], axis=0).astype(BF16)
+        features[:, here] = jnp.where(cover[7:8, here] > 0.5, placed, text[:, here])
+        part = pl.ds(k * wide, wide)
+        stores.append(
+            pltpu.make_async_copy(features.at[:, part], features_hbm.at[:, part], store_sem.at[1 + k])
+        )
+        stores[-1].start()
 
     phase('col_wait')
     pltpu.make_async_copy(col_in, col_in, col_recv).wait()
@@ -578,7 +643,11 @@
     total = jnp.sum(col_in[...].astype(F32), axis=0)
     tail = total[each : each + each // 2]
     tail = jnp.concatenate([tail[:, :over], tail[:, over : 2 * over]], axis=0)
-    grad_ref[...] = jnp.concatenate([total[:each], tail], axis=1)
+    grad[...] = jnp.concatenate([total[:each], tail], axis=1)
+    stores.append(pltpu.make_async_copy(grad, grad_hbm, store_sem.at[0]))
+    stores[-1].start()
+    for store in stores:
+        store.wait()
     phase(None)
 
 
@@ -614,7 +683,7 @@
     slots = ndp * g.length
     room = LANES // g.per_t
     half = max(ny // 2, 1)
-    hbm, vmem = pl.BlockSpec(memory_space=pl.ANY), pl.BlockSpec(memory_space=pltpu.VMEM)
+    hbm = pl.BlockSpec(memory_space=pl.ANY)
     dma = pltpu.SemaphoreType.DMA
     ring = (g.chunks, ny, rows, g.width)
     packets = (ndp, 2 * g.length, LANES)
@@ -631,8 +700,8 @@
         pltpu.VMEM((1,) + ln_bias.shape, F32),
         pltpu.VMEM(ring, BF16),
         pltpu.VMEM(ring, BF16),
-        pltpu.VMEM((ny, 2, rows // 2, rows), BF16),
-        pltpu.VMEM((2, ny, rows // 2, rows), BF16),
+        pltpu.VMEM((ny, 2, 2, rows // 4, rows), BF16),
+        pltpu.VMEM((2, 2, ny, rows // 4, rows), BF16),
         pltpu.VMEM((slots, seq), BF16),
         pltpu.VMEM((slots, cols), BF16),
         pltpu.VMEM((d, g.width), F32),
@@ -640,8 +709,8 @@
         pltpu.VMEM(packets, BF16),
         pltpu.VMEM(packets, BF16),
         pltpu.VMEM((2, LANES, cols), BF16),
-        pltpu.VMEM(packets, BF16),
-        pltpu.VMEM(packets, BF16),
+        pltpu.VMEM((ndp, g.length, LANES), BF16),
+        pltpu.VMEM((ndp, g.length, LANES), BF16),
         pltpu.VMEM((g.chunks, rows, g.width), F32),
         pltpu.VMEM((nx, d // nx, LANES), F32),
         pltpu.VMEM((nx, d // nx, LANES), F32),
@@ -650,6 +719,16 @@
         pltpu.VMEM((nx - 1, d // nx, LANES), BF16),
         pltpu.VMEM((g.per_x, g.per_t, room, LANES), BF16),
         pltpu.VMEM((g.nz, room, LANES), BF16),
+        pltpu.VMEM(text_rows.shape, BF16),
+        pltpu.VMEM((g.each, rows), F32),
+        pltpu.VMEM((ndp, 2, LANES), F32),
+        pltpu.VMEM((ndp, 2, LANES), F32),
+        pltpu.VMEM((slots, seq), BF16),
+        pltpu.VMEM((ndp, cols), BF16),
+        pltpu.VMEM((8, seq), F32),
+        dma((1 + seq // g.seq_block,)),
+        dma,
+        dma,
         pltpu.SemaphoreType.REGULAR((8,)),
         dma((10,)),
         dma((2, half, 2 * g.chunks)),
@@ -658,8 +737,8 @@
         dma((2, half, 2 * g.chunks)),
         dma((2,)),
         dma((2,)),
-        dma((2,)),
-        dma((2,)),
+        dma((3,)),
+        dma((3,)),
         dma((nx,)),
         dma((nx,)),
         dma((nx,)),
@@ -674,7 +753,7 @@
             jax.ShapeDtypeStruct((g.each, rows), F32),
         ),
         in_specs=[hbm] * 10,
-        out_specs=(vmem, vmem),
+        out_specs=(hbm, hbm),
         scratch_shapes=scratch,
         compiler_params=pltpu.CompilerParams(collective_id=0, has_side_effects=True),
     )(

time: 83 us -> 78.6 us (0.947)
  Pallas kernels: 79.1 us -> 74.7 us
    pallas_call x1, Pallas kernels: 79.1 us -> 74.7 us  [shards(): pl.pallas_call(functools.partial(kernel, g), out_shape=(jax.ShapeDtypeStr...]
where the time goes in v3:
time: 78.6 us; the launch traced here: 78.3 us
  Pallas kernels  74.7 us (95%)
  local copies, waits for them, and re-layouts  2.98 us (4%)
    pallas_call x1, Pallas kernels, shards(): pl.pallas_call(functools.partial(kernel, g), out_shape=(jax.ShapeDtypeStr...  74.7 us
    unnamed x2, local copies, waits for them, and re-layouts  2.98 us

profile of v3, /device:TPU:68, one launch (start us, length us, event | category | flops | bytes accessed | tf_op | source)
XLA Modules:
  0.0 78.3 jit_solution(12595360237177660603)
XLA Ops:
  0.6 74.7 %shard_map.113 = (bf16[160,768]{1,0:T(8,128)(2,1)}, f32[10,160]{1,0:T(8,128)}) custom-call(bf16[160,384]{1,0:T(8,128)(2,1)} %patches_hbm.1, bf16[160,768]{1,0:T(8,128)(2,1)} %text_hbm.1, bf16[160,768]{1,0:T(8,128)(2,1)} %cot_hbm.1, bf16[3,160,1280]{2,1,0:T(8,128)(2,1)} %wqkv_hbm.1, bf16[160,1280]{1,0:T(8,128)(2,1)} %wout_hbm.1, s32[48]{0:T(128)} %lengths_hbm.1, ...), custom_call_target="tpu_custom_call" | custom-call | tf_op jit(solution)/shard_map/pallas_call | solution.py:749
  75.4 1.7 %copy.14 = bf16[160,768]{1,0:T(8,128)(2,1)} copy(bf16[160,768]{1,0:T(8,128)(2,1)} %get-tuple-element.8) | data formatting | bytes 491520
  77.0 1.3 %copy.15 = f32[160,10]{0,1:T(8,128)} copy(f32[160,10]{0,1:T(8,128)} %bitcast.1) | data formatting | bytes 12800
